TPU v7x, 256 devices: a whole 4x4x8 slice. The times are simulated.
256 devices in a mesh: section: 2 (over x_hi), row: 8 (over y, x_lo), col: 16 (over z, core).
Axes of the slice: x: 4 (x_hi: 2, x_lo: 2; x = x_hi * 2 + x_lo), y: 4, z: 8, core: 2. Of those that a mesh axis runs over, the one named last changes fastest.
Arguments:
- images: bfloat16 [2, 8, 48, 128, 256], P('section', None, None, 'row', 'col'), may hold values from -6 to 6
- stem_first: bfloat16 [48, 256], replicated, may hold values from -0.875 to 0.875
- stem_conv: bfloat16 [3, 3, 256, 256], replicated, may hold values from -0.125 to 0.125
- patch_weight: bfloat16 [4096, 1024], P('col'), may hold values from -0.09375 to 0.09375
- position: bfloat16 [64, 32, 1024], P('col', 'row'), may hold values from -6 to 6
- gain_attn: float32 [1024], replicated, may hold values from 0.1 to 1.9
- w_qkv: bfloat16 [3, 1024, 1024], P(None, None, 'col'), may hold values from -0.5 to 0.5
- w_out: bfloat16 [1024, 1024], P('col'), may hold values from -0.1875 to 0.1875
- gain_mlp: float32 [1024], replicated, may hold values from 0.1 to 1.9
- w_up: bfloat16 [1024, 4096], P(None, 'col'), may hold values from -0.1875 to 0.1875
- w_down: bfloat16 [4096, 1024], P('col'), may hold values from -0.09375 to 0.09375
Outputs:
- encoded: bfloat16 [2, 8, 64, 32, 1024], P('section', 'row', 'col')
All inputs are finite; a program needn't handle non-finite values.
Results may differ from a plain program's by a relative error of at most 0.024.
The roundings to bfloat16 on the way count: a program that leaves them out, or rounds other values in their place, can miss the bound.
Values may be sent and summed in bfloat16 or wider, within the bound.
No kernel may reach another device: no remote copies, remote signals or barrier semaphores. Data moves between devices by JAX's collectives and lax.ppermute only.
A program may use at most 64 MiB of HBM per device.

v0:
```python
import math
import jax
import jax.numpy as jnp
from jax import lax
from jax.sharding import PartitionSpec as P

HD = 64


def with_halo(block, sides, width):
    for axis, dim in sides:
        count = lax.axis_size(axis)
        forward = [(i, i + 1) for i in range(count - 1)]
        backward = [(target, source) for source, target in forward]
        low = lax.ppermute(
            lax.slice_in_dim(block, block.shape[dim] - width, None, axis=dim), axis, forward
        )
        high = lax.ppermute(lax.slice_in_dim(block, 0, width, axis=dim), axis, backward)
        block = jnp.concatenate([low, block, high], axis=dim)
    return block


def passed_along(value, axis, steps):
    count = lax.axis_size(axis)
    pairs = [(source, (source + steps) % count) for source in range(count)]
    return lax.ppermute(value, axis, pairs)


def layer_norm(vectors, gain_vec):
    row_mean = jnp.mean(vectors, axis=-1, keepdims=True)
    center = vectors - row_mean
    spread = jnp.mean(center * center, axis=-1, keepdims=True)
    return center * lax.rsqrt(spread + 1e-06) * gain_vec


def stem_features(images, stem_first, stem_conv):
    pixels = images[0]
    first_map = jnp.einsum("ikhw,kc->ihwc", pixels, stem_first, preferred_element_type=jnp.float32)
    stem_maps = jnp.maximum(first_map, 0.0).astype(jnp.bfloat16)
    padded = with_halo(stem_maps, (("row", 1), ("col", 2)), 1)
    img_count, height, tile_width, channels = stem_maps.shape
    summed = stem_maps.astype(jnp.float32)
    for offset_a in range(3):
        for offset_b in range(3):
            window = padded[:, offset_a : offset_a + height, offset_b : offset_b + tile_width, :]
            summed = summed + jnp.einsum(
                "ihwc,cd->ihwd",
                window,
                stem_conv[offset_a, offset_b],
                preferred_element_type=jnp.float32,
            )
    deep_maps = jnp.maximum(summed, 0.0).astype(jnp.bfloat16)
    blocks = deep_maps.reshape(img_count, height // 4, 4, tile_width // 4, 4, channels).transpose(
        0, 3, 1, 2, 4, 5
    )
    return blocks.reshape(img_count, tile_width // 4, height // 4, 16 * channels)


def on_device(
    images,
    stem_first,
    stem_conv,
    patch_weight,
    position,
    gain_attn,
    w_qkv,
    w_out,
    gain_mlp,
    w_up,
    w_down,
):
    features = stem_features(images, stem_first, stem_conv)
    img_count, cols_here, rows_here, feat_width = features.shape
    model_width = patch_weight.shape[1]
    flat_local = features.reshape(-1, feat_width)
    embedded = jnp.dot(
        flat_local,
        lax.all_gather(patch_weight, "col", axis=0, tiled=True),
        preferred_element_type=jnp.float32,
    )
    local_tokens = (
        embedded.reshape(img_count, cols_here, rows_here, model_width)
        + position.astype(jnp.float32)[None]
    ).astype(jnp.bfloat16)
    arrived = passed_along(local_tokens, "section", 1)
    token_image = lax.all_to_all(arrived, "row", split_axis=0, concat_axis=2, tiled=True)
    tokens_in = token_image.reshape(-1, model_width)
    residual = tokens_in.astype(jnp.float32)
    normed = layer_norm(residual, gain_attn).astype(jnp.bfloat16)
    projected = jnp.einsum(
        "td,kdh->kth",
        lax.all_gather(normed, "col", axis=0, tiled=True),
        w_qkv,
        preferred_element_type=jnp.float32,
    ).astype(jnp.bfloat16)
    token_count = projected.shape[1]
    local_heads = w_out.shape[0] // HD
    split_heads = projected.reshape(3, token_count, local_heads, HD).transpose(0, 2, 1, 3)
    key_heads = split_heads[1]
    value_heads = split_heads[2]
    block_rows = math.gcd(token_count, 512)
    query_blocks = (
        split_heads[0]
        .reshape(local_heads, token_count // block_rows, block_rows, HD)
        .transpose(1, 0, 2, 3)
    )

    def attend(query_block):
        scores = jnp.einsum(
            "hqd,hkd->hqk", query_block, key_heads, preferred_element_type=jnp.float32
        ) * HD ** (-0.5)
        row_peak = jnp.max(scores, axis=-1, keepdims=True)
        expo = jnp.exp(scores - row_peak)
        prob_rows = (expo / jnp.sum(expo, axis=-1, keepdims=True)).astype(jnp.bfloat16)
        return jnp.einsum(
            "hqk,hkd->hqd", prob_rows, value_heads, preferred_element_type=jnp.float32
        ).astype(jnp.bfloat16)

    attended = lax.map(attend, query_blocks)
    mixed_heads = attended.transpose(0, 2, 1, 3).reshape(token_count, local_heads * HD)
    row_slice = mixed_heads
    after = residual + lax.psum_scatter(
        jnp.dot(row_slice, w_out, preferred_element_type=jnp.float32).astype(jnp.bfloat16),
        "col",
        scatter_dimension=0,
        tiled=True,
    ).astype(jnp.float32)
    normed_mlp = layer_norm(after, gain_mlp).astype(jnp.bfloat16)
    hidden = jax.nn.gelu(
        jnp.dot(
            lax.all_gather(normed_mlp, "col", axis=0, tiled=True),
            w_up,
            preferred_element_type=jnp.float32,
        ),
        approximate=True,
    ).astype(jnp.bfloat16)
    row_slice = hidden
    encoded = (
        after
        + lax.psum_scatter(
            jnp.dot(row_slice, w_down, preferred_element_type=jnp.float32).astype(jnp.bfloat16),
            "col",
            scatter_dimension=0,
            tiled=True,
        ).astype(jnp.float32)
    ).astype(jnp.bfloat16)
    return encoded.reshape(1, 1, cols_here, -1, model_width)


def solution(mesh):
    placed = (
        P("section", None, None, "row", "col"),
        P(),
        P(),
        P("col", None),
        P("col", "row", None),
        P(),
        P(None, None, "col"),
        P("col", None),
        P(),
        P(None, "col"),
        P("col", None),
    )
    return jax.shard_map(
        on_device,
        mesh=mesh,
        in_specs=placed,
        out_specs=P("section", "row", "col", None, None),
        check_vma=False,
    )
```

profile of v0, /device:TPU:2, one launch (start us, length us, event | category | flops | bytes accessed | tf_op | source)
XLA Modules:
  0.0 342.6 jit_solution(3398416995939762517)
XLA Ops:
  7.3 1.4 maximum_convert_fusion.1
  8.8 3.5 %collective-permute-start = (bf16[8,1,16,256]{3,2,1,0:T(8,128)(2,1)S(1)}, bf16[8,1,16,256]{3,2,1,0:T(8,128)(2,1)S(1)}, u32[]{:S(2)}, u32[]{:S(2)}) collective-permute-start(bf16[8,1,16,256]{3,2,1,0:T(8,128)(2,1)S(1)} %get-tuple-element.64), channel_id=1, source_target_pairs={{0,16},{16,32},{32,48},{48,64},{64,80},{80,96},{96,112},{1,17},{17... | collective-permute-start | bytes 196616 | tf_op jit(solution)/shard_map/ppermute | solution.py:15
  12.3 2.4 collective-permute-start.1
  15.1 4.2 %collective-permute-done.1 = bf16[8,1,16,256]{3,2,1,0:T(8,128)(2,1)S(1)} collective-permute-done((bf16[8,1,16,256]{3,2,1,0:T(8,128)(2,1)S(1)}, bf16[8,1,16,256]{3,2,1,0:T(8,128)(2,1)S(1)}, u32[]{:S(2)}, u32[]{:S(2)}) %collective-permute-start.1) | collective-permute-done | bytes 65568 | tf_op jit(solution)/shard_map/ppermute | solution.py:18
  19.6 1.3 collective-permute-start.2
  20.9 1.3 collective-permute-start.3
  23.0 3.2 collective-permute-done.3
  26.3 1.2 pad_maximum_fusion
  29.7 1.2 maximum_convert_fusion
  32.3 35.9 %all-gather.4.cloned.1.call-done = bf16[4096,1024]{1,0:T(8,128)(2,1)} async-done(((bf16[256,1024]{1,0:T(8,128)(2,1)}), bf16[4096,1024]{1,0:T(8,128)(2,1)}) %all-gather.4.cloned.1.call-update) | async-done | bytes 8388624 | tf_op jit(solution)/shard_map/all_gather | solution.py:78
  68.2 4.6 %fusion.25 = bf16[8,4,4,1024]{3,0,2,1:T(8,128)(2,1)S(1)} fusion(bf16[8,4,4,4096]{3,0,2,1:T(8,128)(2,1)S(1)} %bitcast.143, bf16[4096,1024]{1,0:T(8,128)(2,1)} %all-gather.4.cloned.1.call-done, f32[4,4,1024]{2,1,0:T(4,128)S(1)} %convert_element_type.74), kind=kOutput, calls=%fused_computation.33 | convolution fusion | flops 1074003968 | bytes 9764864 | tf_op jit(solution)/shard_map/dot_general | solution.py:76
  72.8 2.2 collective-permute-start.4
  75.0 7.9 %collective-permute-done.4 = bf16[8,4,4,1024]{3,0,2,1:T(8,128)(2,1)S(1)} collective-permute-done((bf16[8,4,4,1024]{3,0,2,1:T(8,128)(2,1)S(1)}, bf16[8,4,4,1024]{3,0,2,1:T(8,128)(2,1)S(1)}, u32[]{:S(2)}, u32[]{:S(2)}) %collective-permute-start.4) | collective-permute-done | bytes 262176 | tf_op jit(solution)/shard_map/ppermute | solution.py:26
  83.1 11.7 %all_to_all.4 = bf16[8,4,4,1024]{3,2,1,0:T(4,128)(2,1)S(1)} all-to-all(bf16[8,4,4,1024]{3,2,1,0:T(4,128)(2,1)S(1)} %copy.25), channel_id=1, replica_groups=mesh['section'=2,'row'=8,'col'=16] {'row'}, dimensions={0} | all-to-all | bytes 524288 | tf_op jit(solution)/shard_map/all_to_all | solution.py:86
  97.4 40.1 %all-gather.6.cloned.1.call-done = bf16[2048,1024]{1,0:T(8,128)(2,1)} async-done(((bf16[128,1024]{1,0:T(8,128)(2,1)}), bf16[2048,1024]{1,0:T(8,128)(2,1)}) %all-gather.6.cloned.1.call-update) | async-done | bytes 4194320 | tf_op jit(solution)/shard_map/all_gather | solution.py:92
  137.6 3.7 %fusion.88 = f32[2048,192]{0,1:S(1)} fusion(bf16[2048,1024]{1,0:T(8,128)(2,1)} %all-gather.6.cloned.1.call-done, bf16[1024,192]{0,1:T(8,128)(2,1)S(1)} %bitcast.148), kind=kOutput, calls=%fused_computation.105 | convolution fusion | flops 805306368 | bytes 6160384
  142.3 11.1 %while.10 = (s32[]{:T(128)}, bf16[4,1,512,64]{2,3,1,0:T(8,128)(2,1)S(1)}, bf16[4,1,512,64]{3,2,1,0:T(8,128)(2,1)S(1)}, bf16[1,2048,64]{2,1,0:T(8,128)(2,1)S(1)}, bf16[1,2048,64]{2,1,0:T(8,128)(2,1)S(1)}, /*index=5*/s32[]{:T(128)}) while((s32[]{:T(128)}, bf16[4,1,512,64]{2,3,1,0:T(8,128)(2,1)S(1)}, bf16[4,1,512,64]{3,2,1,0:T(8,128)(2,1)S(1)}, ...), condition=%wide.region_5.6_spmd, body=%wide.region_2.5_spmd.sunk | while | flops 277904384 | bytes 13838413 | solution.py:119
  153.8 3.2 convolution_convert_fusion.1
  157.1 61.9 %reduce-scatter.3.cloned.1.call-done = bf16[128,1024]{1,0:T(8,128)(2,1)} async-done(((bf16[2048,1024]{1,0:T(8,128)(2,1)}), bf16[128,1024]{1,0:T(8,128)(2,1)}) %reduce-scatter.3.cloned.1.call-update) | async-done | bytes 262160 | tf_op jit(solution)/shard_map/reduce_scatter | solution.py:122
  221.2 1.8 multiply_convert_fusion
  223.1 40.5 %all-gather.8.cloned.1.call-done = bf16[2048,1024]{1,0:T(8,128)(2,1)} async-done(((bf16[128,1024]{1,0:T(8,128)(2,1)}), bf16[2048,1024]{1,0:T(8,128)(2,1)}) %all-gather.8.cloned.1.call-update) | async-done | bytes 4194320 | tf_op jit(solution)/shard_map/all_gather | solution.py:131
  263.6 8.5 %convolution_convert_fusion = bf16[2048,1024]{1,0:T(8,128)(2,1)} fusion(bf16[256,1024]{1,0:T(8,128)(2,1)S(1)} %copy-done, bf16[2048,1024]{1,0:T(8,128)(2,1)} %all-gather.8.cloned.1.call-done, bf16[1024,256]{1,0:T(8,128)(2,1)S(1)} %copy-done.8), kind=kOutput, calls=%fused_computation.17 | convolution fusion | flops 2154299392 | bytes 9437184 | tf_op jit(solution)/shard_map/dot_general | solution.py:141
  272.1 62.1 %reduce-scatter.5.cloned.1.call-done = bf16[128,1024]{1,0:T(8,128)(2,1)} async-done(((bf16[2048,1024]{1,0:T(8,128)(2,1)}), bf16[128,1024]{1,0:T(8,128)(2,1)}) %reduce-scatter.5.cloned.1.call-update) | async-done | bytes 262160 | tf_op jit(solution)/shard_map/reduce_scatter | solution.py:140
  334.3 1.7 add_convert_fusion
  (83 shorter events, 23.4 us)
Async XLA Ops:
  6.5 257.1 %copy-start = (bf16[256,1024]{1,0:T(8,128)(2,1)S(1)}, bf16[256,1024]{1,0:T(8,128)(2,1)}, u32[]{:S(2)}) copy-start(bf16[256,1024]{1,0:T(8,128)(2,1)} %param.23) | copy-start | bytes 1572868
  6.5 8.1 %copy-start.2 = (bf16[3,3,256,256]{3,2,1,0:T(8,128)(2,1)S(1)}, bf16[3,3,256,256]{3,2,1,0:T(8,128)(2,1)}, u32[]{:S(2)}) copy-start(bf16[3,3,256,256]{3,2,1,0:T(8,128)(2,1)} %param.15) | copy-start | bytes 3538948
  6.5 61.7 %all-gather.4.cloned.1.call-start = ((), (), s32[]{:S(2)}) async-start(), calls=%async_computation.3 | async-start | bytes 8912896 | tf_op jit(solution)/shard_map/all_gather | solution.py:78
  7.3 130.3 %all-gather.6.cloned.1.call-start = ((), (), s32[]{:S(2)}) async-start(), calls=%async_computation.4 | async-start | bytes 4456448 | tf_op jit(solution)/shard_map/all_gather | solution.py:92
  8.8 6.3 %copy-start.5 = (bf16[4,4,1024]{2,1,0:T(4,128)(2,1)S(1)}, bf16[4,4,1024]{2,1,0:T(4,128)(2,1)}, u32[]{:S(2)}) copy-start(bf16[4,4,1024]{2,1,0:T(4,128)(2,1)} %param.17) | copy-start | bytes 98308
  8.8 6.3 %collective-permute-start = (bf16[8,1,16,256]{3,2,1,0:T(8,128)(2,1)S(1)}, bf16[8,1,16,256]{3,2,1,0:T(8,128)(2,1)S(1)}, u32[]{:S(2)}, u32[]{:S(2)}) collective-permute-start(bf16[8,1,16,256]{3,2,1,0:T(8,128)(2,1)S(1)} %get-tuple-element.64), channel_id=1, source_target_pairs={{0,16},{16,32},{32,48},{48,64},{64,80},{80,96},{96,112},{1,17},{17... | collective-permute-start | bytes 196616 | tf_op jit(solution)/shard_map/ppermute | solution.py:15
  12.3 7.1 %collective-permute-start.1 = (bf16[8,1,16,256]{3,2,1,0:T(8,128)(2,1)S(1)}, bf16[8,1,16,256]{3,2,1,0:T(8,128)(2,1)S(1)}, u32[]{:S(2)}, u32[]{:S(2)}) collective-permute-start(bf16[8,1,16,256]{3,2,1,0:T(8,128)(2,1)S(1)} %get-tuple-element.65), channel_id=1, source_target_pairs={{16,0},{32,16},{48,32},{64,48},{80,64},{96,80},{112,96},{17,1},{33... | collective-permute-start | bytes 196616 | tf_op jit(solution)/shard_map/ppermute | solution.py:18
  19.6 3.5 %collective-permute-start.2 = (bf16[8,18,1,256]{3,2,1,0:T(2,128)(2,1)S(1)}, bf16[8,18,1,256]{3,2,1,0:T(2,128)(2,1)S(1)}, u32[]{:S(2)}, u32[]{:S(2)}) collective-permute-start(bf16[8,18,1,256]{3,2,1,0:T(2,128)(2,1)S(1)} %get-tuple-element.63), channel_id=1, source_target_pairs={{0,1},{1,2},{2,3},{3,4},{4,5},{5,6},{6,7},{7,8},{8,9},{9,10},{10,1... | collective-permute-start | bytes 221192 | tf_op jit(solution)/shard_map/ppermute | solution.py:15
  20.9 5.4 %collective-permute-start.3 = (bf16[8,18,1,256]{3,2,1,0:T(2,128)(2,1)S(1)}, bf16[8,18,1,256]{3,2,1,0:T(2,128)(2,1)S(1)}, u32[]{:S(2)}, u32[]{:S(2)}) collective-permute-start(bf16[8,18,1,256]{3,2,1,0:T(2,128)(2,1)S(1)} %get-tuple-element.62), channel_id=1, source_target_pairs={{1,0},{2,1},{3,2},{4,3},{5,4},{6,5},{7,6},{8,7},{9,8},{10,9},{11,1... | collective-permute-start | bytes 221192 | tf_op jit(solution)/shard_map/ppermute | solution.py:18
  72.8 10.0 %collective-permute-start.4 = (bf16[8,4,4,1024]{3,0,2,1:T(8,128)(2,1)S(1)}, bf16[8,4,4,1024]{3,0,2,1:T(8,128)(2,1)S(1)}, u32[]{:S(2)}, u32[]{:S(2)}) collective-permute-start(bf16[8,4,4,1024]{3,0,2,1:T(8,128)(2,1)S(1)} %fusion.25), channel_id=1, source_target_pairs={{0,128},{128,0},{1,129},{129,1},{2,130},{130,2},{3,131},{131,3},{4... | collective-permute-start | bytes 786440 | tf_op jit(solution)/shard_map/ppermute | solution.py:26
  83.1 13.2 %copy-start.6 = (f32[1024]{0:T(1024)S(1)}, f32[1024]{0:T(1024)}, u32[]{:S(2)}) copy-start(f32[1024]{0:T(1024)} %param.18) | copy-start | bytes 12292
  95.3 42.3 %copy-start.3 = (bf16[3,1024,64]{1,2,0:T(8,128)(2,1)S(1)}, bf16[3,1024,64]{1,2,0:T(8,128)(2,1)}, u32[]{:S(2)}) copy-start(bf16[3,1024,64]{1,2,0:T(8,128)(2,1)} %param.19) | copy-start | bytes 1179652
  97.2 121.8 %reduce-scatter.3.cloned.1.call-start = ((), (), s32[]{:S(2)}) async-start(), calls=%async_computation.5 | async-start | bytes 4456448 | tf_op jit(solution)/shard_map/reduce_scatter | solution.py:122
  142.3 11.4 %copy-start.4 = (bf16[64,1024]{1,0:T(8,128)(2,1)S(1)}, bf16[64,1024]{1,0:T(8,128)(2,1)}, u32[]{:S(2)}) copy-start(bf16[64,1024]{1,0:T(8,128)(2,1)} %param.20) | copy-start | bytes 393220
  157.0 64.2 %copy-start.7 = (f32[1024]{0:T(1024)S(1)}, f32[1024]{0:T(1024)}, u32[]{:S(2)}) copy-start(f32[1024]{0:T(1024)} %param.21) | copy-start | bytes 12292
  157.0 106.6 %copy-start.8 = (bf16[1024,256]{1,0:T(8,128)(2,1)S(1)}, bf16[1024,256]{1,0:T(8,128)(2,1)}, u32[]{:S(2)}) copy-start(bf16[1024,256]{1,0:T(8,128)(2,1)} %param.22) | copy-start | bytes 1572868
  157.0 106.6 %all-gather.8.cloned.1.call-start = ((), (), s32[]{:S(2)}) async-start(), calls=%async_computation.6 | async-start | bytes 4456448 | tf_op jit(solution)/shard_map/all_gather | solution.py:131
  223.1 111.2 %reduce-scatter.5.cloned.1.call-start = ((), (), s32[]{:S(2)}) async-start(), calls=%async_computation.7 | async-start | bytes 4456448 | tf_op jit(solution)/shard_map/reduce_scatter | solution.py:140
  272.1 62.2 %copy-start.1 = (bf16[128,1024]{1,0:T(8,128)(2,1)S(1)}, bf16[128,1024]{1,0:T(8,128)(2,1)}, u32[]{:S(2)}) copy-start(bf16[128,1024]{1,0:T(8,128)(2,1)} %reduce-scatter.3.cloned.1.call-done) | copy-start | bytes 786436
Sparse Core Ops, SparseCore 0:
  9.2 58.9 all-gather.3
  97.3 40.1 all-gather.5
  157.1 61.7 reduce-scatter.2
  223.2 40.3 all-gather.7
  272.3 61.9 reduce-scatter.4
where the time goes:
time: 343 us
  waiting for transfers between devices  257 us (75%)
  matrix products  34 us (10%)
  between operations  13.4 us (4%)
  other arithmetic  12 us (3%)
  blocking collectives  11.7 us (3%)
  starting transfers between devices  10.9 us (3%)
  local copies, waits for them, and re-layouts  3.78 us (1%)
    reduce_scatter x1, waiting for transfers between devices, on_device(): lax.psum_scatter(jnp.dot(row_slice, w_down, preferred_element_type=jnp.fl...  62.1 us
    reduce_scatter x1, waiting for transfers between devices, on_device(): lax.psum_scatter(jnp.dot(row_slice, w_out, preferred_element_type=jnp.flo...  61.9 us
    all_gather x1, waiting for transfers between devices, on_device(): lax.all_gather(normed_mlp, 'col', axis=0, tiled=True)  40.5 us
    all_gather x1, waiting for transfers between devices, on_device(): lax.all_gather(normed, 'col', axis=0, tiled=True)  40.1 us
    all_gather x1, waiting for transfers between devices, on_device(): lax.all_gather(patch_weight, 'col', axis=0, tiled=True)  35.9 us
    all_to_all x1, blocking collectives, on_device(): lax.all_to_all(arrived, 'row', split_axis=0, concat_axis=2, tiled=True)  11.7 us
    dot_general x1, matrix products, on_device(): jnp.dot(row_slice, w_down, preferred_element_type=jnp.float32)  8.49 us
    ppermute x1, waiting for transfers between devices, passed_along(): return lax.ppermute(value, axis, pairs)  7.88 us
  transfers between devices with their start and end apart: 10, of which 8 were waited for; matrix products, arithmetic and copies ran while one was open for 3% of the time, Pallas kernels for 0%

commit v1 on v0

--- a/solution.py
+++ b/solution.py
@@ -5,6 +5,11 @@
 from jax.sharding import PartitionSpec as P
 
 HD = 64
+
+
+def swapped_in(x, axis, dim):
+    sent = jnp.stack([x] * lax.axis_size(axis))
+    return jnp.concatenate(lax.all_to_all(sent, axis, 0, 0), axis=dim)
 
 
 def with_halo(block, sides, width):
@@ -74,9 +79,7 @@
     model_width = patch_weight.shape[1]
     flat_local = features.reshape(-1, feat_width)
     embedded = jnp.dot(
-        flat_local,
-        lax.all_gather(patch_weight, "col", axis=0, tiled=True),
-        preferred_element_type=jnp.float32,
+        flat_local, swapped_in(patch_weight, "col", 0), preferred_element_type=jnp.float32
     )
     local_tokens = (
         embedded.reshape(img_count, cols_here, rows_here, model_width)

time: 343 us -> 486 us (1.42)
  waiting for transfers between devices: 257 us -> 386 us
  starting transfers between devices: 10.9 us -> 19.7 us
  local copies, waits for them, and re-layouts: 3.78 us -> 9.19 us
    all_to_all x0 -> x1, waiting for transfers between devices: none -> 160 us  [swapped_in(): return jnp.concatenate(lax.all_to_all(sent, axis, 0, 0), axis=dim)]
    all_gather x1 -> x0, waiting for transfers between devices: 35.9 us -> none  [on_device(): lax.all_gather(patch_weight, 'col', axis=0, tiled=True)]
    all_to_all x0 -> x1, starting transfers between devices: none -> 8.75 us  [swapped_in(): return jnp.concatenate(lax.all_to_all(sent, axis, 0, 0), axis=dim)]
    all_gather x1, waiting for transfers between devices: 40.1 us -> 48.4 us  [on_device(): lax.all_gather(normed, 'col', axis=0, tiled=True)]
    another operation x0 -> x1, local copies, waits for them, and re-layouts: none -> 5.41 us  [swapped_in(): sent = jnp.stack([x] * lax.axis_size(axis))]
  transfers between devices with their start and end apart: 10 -> 10, of which waited for: 8 -> 8; matrix products, arithmetic and copies ran while one was open for 3% -> 2% of each run, Pallas kernels for 0% -> 0%
where the time goes in v1:
time: 486 us
  waiting for transfers between devices  386 us (79%)
  matrix products  32.9 us (7%)
  starting transfers between devices  19.7 us (4%)
  between operations  13.5 us (3%)
  other arithmetic  12 us (2%)
  blocking collectives  11.8 us (2%)
  local copies, waits for them, and re-layouts  9.19 us (2%)
    all_to_all x1, waiting for transfers between devices, swapped_in(): return jnp.concatenate(lax.all_to_all(sent, axis, 0, 0), axis=dim)  160 us
    reduce_scatter x1, waiting for transfers between devices, on_device(): lax.psum_scatter(jnp.dot(row_slice, w_down, preferred_element_type=jnp.fl...  62 us
    reduce_scatter x1, waiting for transfers between devices, on_device(): lax.psum_scatter(jnp.dot(row_slice, w_out, preferred_element_type=jnp.flo...  61.9 us
    all_gather x1, waiting for transfers between devices, on_device(): lax.all_gather(normed, 'col', axis=0, tiled=True)  48.4 us
    all_gather x1, waiting for transfers between devices, on_device(): lax.all_gather(normed_mlp, 'col', axis=0, tiled=True)  40.7 us
    all_to_all x1, blocking collectives, on_device(): lax.all_to_all(arrived, 'row', split_axis=0, concat_axis=2, tiled=True)  11.8 us
  transfers between devices with their start and end apart: 10, of which 8 were waited for; matrix products, arithmetic and copies ran while one was open for 2% of the time, Pallas kernels for 0%

profile of v1, /device:TPU:2, one launch (start us, length us, event | category | flops | bytes accessed | tf_op | source)
XLA Modules:
  0.0 485.7 jit_solution(3135001879385161445)
XLA Ops:
  6.5 5.4 %stack.2 = bf16[16,256,1024]{2,1,0:T(8,128)(2,1)} broadcast(bf16[256,1024]{1,0:T(8,128)(2,1)} %param.16), dimensions={1,2} | broadcast | bytes 8912896 | tf_op jit(solution)/shard_map/stack | solution.py:11
  12.0 8.8 %all-to-all-start = ((bf16[16,256,1024]{2,1,0:T(8,128)(2,1)}), bf16[16,256,1024]{2,1,0:T(8,128)(2,1)}, u32[]{:S(2)}, u32[]{:S(2)}) async-start(bf16[16,256,1024]{2,1,0:T(8,128)(2,1)} %stack.2), calls=%async_computation | async-start | bytes 16777216 | tf_op jit(solution)/shard_map/all_to_all | solution.py:12
  21.2 3.5 collective-permute-start
  24.7 2.4 collective-permute-start.1
  27.6 4.2 collective-permute-done.1
  32.0 1.3 collective-permute-start.2
  33.3 1.3 collective-permute-start.3
  35.5 3.2 collective-permute-done.3
  42.0 1.2 maximum_convert_fusion
  44.7 160.3 %all-to-all-done = bf16[16,256,1024]{2,1,0:T(8,128)(2,1)} async-done(((bf16[16,256,1024]{2,1,0:T(8,128)(2,1)}), bf16[16,256,1024]{2,1,0:T(8,128)(2,1)}, u32[]{:S(2)}, u32[]{:S(2)}) %all-to-all-start) | async-done | bytes 8388640 | tf_op jit(solution)/shard_map/all_to_all | solution.py:12
  204.9 4.6 fusion.20
  209.6 2.2 collective-permute-start.4
  211.8 5.8 %collective-permute-done.4 = bf16[8,4,4,1024]{3,0,2,1:T(8,128)(2,1)S(1)} collective-permute-done((bf16[8,4,4,1024]{3,0,2,1:T(8,128)(2,1)S(1)}, bf16[8,4,4,1024]{3,0,2,1:T(8,128)(2,1)S(1)}, u32[]{:S(2)}, u32[]{:S(2)}) %collective-permute-start.4) | collective-permute-done | bytes 262176 | tf_op jit(solution)/shard_map/ppermute | solution.py:31
  217.8 11.8 %all_to_all.14 = bf16[8,4,4,1024]{3,2,1,0:T(4,128)(2,1)S(1)} all-to-all(bf16[8,4,4,1024]{3,2,1,0:T(4,128)(2,1)S(1)} %copy.25), channel_id=1, replica_groups=mesh['section'=2,'row'=8,'col'=16] {'row'}, dimensions={0} | all-to-all | bytes 524288 | tf_op jit(solution)/shard_map/all_to_all | solution.py:89
  232.3 48.4 %all-gather.3.cloned.1.call-done = bf16[2048,1024]{1,0:T(8,128)(2,1)} async-done(((bf16[128,1024]{1,0:T(8,128)(2,1)}), bf16[2048,1024]{1,0:T(8,128)(2,1)}) %all-gather.3.cloned.1.call-update) | async-done | bytes 4194320 | tf_op jit(solution)/shard_map/all_gather | solution.py:95
  280.7 3.7 fusion.81
  285.5 11.1 %while.10 = (s32[]{:T(128)}, bf16[4,1,512,64]{2,3,1,0:T(8,128)(2,1)S(1)}, bf16[4,1,512,64]{3,2,1,0:T(8,128)(2,1)S(1)}, bf16[1,2048,64]{2,1,0:T(8,128)(2,1)S(1)}, bf16[1,2048,64]{2,1,0:T(8,128)(2,1)S(1)}, /*index=5*/s32[]{:T(128)}) while((s32[]{:T(128)}, bf16[4,1,512,64]{2,3,1,0:T(8,128)(2,1)S(1)}, bf16[4,1,512,64]{3,2,1,0:T(8,128)(2,1)S(1)}, ...), condition=%wide.region_5.6_spmd, body=%wide.region_2.5_spmd.sunk | while | flops 277904384 | bytes 13838413 | solution.py:122
  296.9 3.2 convolution_convert_fusion.1
  300.2 61.9 %reduce-scatter.3.cloned.1.call-done = bf16[128,1024]{1,0:T(8,128)(2,1)} async-done(((bf16[2048,1024]{1,0:T(8,128)(2,1)}), bf16[128,1024]{1,0:T(8,128)(2,1)}) %reduce-scatter.3.cloned.1.call-update) | async-done | bytes 262160 | tf_op jit(solution)/shard_map/reduce_scatter | solution.py:125
  364.4 1.8 multiply_convert_fusion
  366.2 40.7 %all-gather.5.cloned.1.call-done = bf16[2048,1024]{1,0:T(8,128)(2,1)} async-done(((bf16[128,1024]{1,0:T(8,128)(2,1)}), bf16[2048,1024]{1,0:T(8,128)(2,1)}) %all-gather.5.cloned.1.call-update) | async-done | bytes 4194320 | tf_op jit(solution)/shard_map/all_gather | solution.py:134
  407.0 8.5 %convolution_convert_fusion = bf16[2048,1024]{1,0:T(8,128)(2,1)} fusion(bf16[256,1024]{1,0:T(8,128)(2,1)S(1)} %copy-done, bf16[2048,1024]{1,0:T(8,128)(2,1)} %all-gather.5.cloned.1.call-done, bf16[1024,256]{1,0:T(8,128)(2,1)S(1)} %copy-done.10), kind=kOutput, calls=%fused_computation.15 | convolution fusion | flops 2154299392 | bytes 9437184 | tf_op jit(solution)/shard_map/dot_general | solution.py:144
  415.5 62.0 %reduce-scatter.5.cloned.1.call-done = bf16[128,1024]{1,0:T(8,128)(2,1)} async-done(((bf16[2048,1024]{1,0:T(8,128)(2,1)}), bf16[128,1024]{1,0:T(8,128)(2,1)}) %reduce-scatter.5.cloned.1.call-update) | async-done | bytes 262160 | tf_op jit(solution)/shard_map/reduce_scatter | solution.py:143
  477.4 1.7 add_convert_fusion
  (87 shorter events, 24.3 us)
Async XLA Ops:
  6.5 400.4 %copy-start = (bf16[256,1024]{1,0:T(8,128)(2,1)S(1)}, bf16[256,1024]{1,0:T(8,128)(2,1)}, u32[]{:S(2)}) copy-start(bf16[256,1024]{1,0:T(8,128)(2,1)} %param.23) | copy-start | bytes 1572868
  11.9 8.8 %copy-start.3 = (bf16[1,8,48,16,16]{2,4,3,1,0:T(8,128)(2,1)S(1)}, bf16[1,8,48,16,16]{2,4,3,1,0:T(8,128)(2,1)}, u32[]{:S(2)}) copy-start(bf16[1,8,48,16,16]{2,4,3,1,0:T(8,128)(2,1)} %param.13) | copy-start | bytes 589828
  11.9 8.8 %copy-start.7 = (bf16[48,256]{1,0:T(8,128)(2,1)S(1)}, bf16[48,256]{1,0:T(8,128)(2,1)}, u32[]{:S(2)}) copy-start(bf16[48,256]{1,0:T(8,128)(2,1)} %param.14) | copy-start | bytes 73732
  12.0 15.1 %copy-start.2 = (bf16[3,3,256,256]{3,2,1,0:T(8,128)(2,1)S(1)}, bf16[3,3,256,256]{3,2,1,0:T(8,128)(2,1)}, u32[]{:S(2)}) copy-start(bf16[3,3,256,256]{3,2,1,0:T(8,128)(2,1)} %param.15) | copy-start | bytes 3538948
  12.0 193.0 %all-to-all-start = ((bf16[16,256,1024]{2,1,0:T(8,128)(2,1)}), bf16[16,256,1024]{2,1,0:T(8,128)(2,1)}, u32[]{:S(2)}, u32[]{:S(2)}) async-start(bf16[16,256,1024]{2,1,0:T(8,128)(2,1)} %stack.2), calls=%async_computation | async-start | bytes 16777216 | tf_op jit(solution)/shard_map/all_to_all | solution.py:12
  20.7 260.0 %all-gather.3.cloned.1.call-start = ((), (), s32[]{:S(2)}) async-start(), calls=%async_computation.4 | async-start | bytes 4456448 | tf_op jit(solution)/shard_map/all_gather | solution.py:95
  21.2 6.3 %copy-start.6 = (bf16[4,4,1024]{2,1,0:T(4,128)(2,1)S(1)}, bf16[4,4,1024]{2,1,0:T(4,128)(2,1)}, u32[]{:S(2)}) copy-start(bf16[4,4,1024]{2,1,0:T(4,128)(2,1)} %param.17) | copy-start | bytes 98308
  21.2 6.3 %collective-permute-start = (bf16[8,1,16,256]{3,2,1,0:T(8,128)(2,1)S(1)}, bf16[8,1,16,256]{3,2,1,0:T(8,128)(2,1)S(1)}, u32[]{:S(2)}, u32[]{:S(2)}) collective-permute-start(bf16[8,1,16,256]{3,2,1,0:T(8,128)(2,1)S(1)} %get-tuple-element.64), channel_id=1, source_target_pairs={{0,16},{16,32},{32,48},{48,64},{64,80},{80,96},{96,112},{1,17},{17... | collective-permute-start | bytes 196616 | tf_op jit(solution)/shard_map/ppermute | solution.py:20
  24.7 7.1 %collective-permute-start.1 = (bf16[8,1,16,256]{3,2,1,0:T(8,128)(2,1)S(1)}, bf16[8,1,16,256]{3,2,1,0:T(8,128)(2,1)S(1)}, u32[]{:S(2)}, u32[]{:S(2)}) collective-permute-start(bf16[8,1,16,256]{3,2,1,0:T(8,128)(2,1)S(1)} %get-tuple-element.65), channel_id=1, source_target_pairs={{16,0},{32,16},{48,32},{64,48},{80,64},{96,80},{112,96},{17,1},{33... | collective-permute-start | bytes 196616 | tf_op jit(solution)/shard_map/ppermute | solution.py:23
  32.0 3.5 collective-permute-start.2
  33.3 5.4 %collective-permute-start.3 = (bf16[8,18,1,256]{3,2,1,0:T(2,128)(2,1)S(1)}, bf16[8,18,1,256]{3,2,1,0:T(2,128)(2,1)S(1)}, u32[]{:S(2)}, u32[]{:S(2)}) collective-permute-start(bf16[8,18,1,256]{3,2,1,0:T(2,128)(2,1)S(1)} %get-tuple-element.62), channel_id=1, source_target_pairs={{1,0},{2,1},{3,2},{4,3},{5,4},{6,5},{7,6},{8,7},{9,8},{10,9},{11,1... | collective-permute-start | bytes 221192 | tf_op jit(solution)/shard_map/ppermute | solution.py:23
  209.6 8.0 %collective-permute-start.4 = (bf16[8,4,4,1024]{3,0,2,1:T(8,128)(2,1)S(1)}, bf16[8,4,4,1024]{3,0,2,1:T(8,128)(2,1)S(1)}, u32[]{:S(2)}, u32[]{:S(2)}) collective-permute-start(bf16[8,4,4,1024]{3,0,2,1:T(8,128)(2,1)S(1)} %fusion.20), channel_id=1, source_target_pairs={{0,128},{128,0},{1,129},{129,1},{2,130},{130,2},{3,131},{131,3},{4... | collective-permute-start | bytes 786440 | tf_op jit(solution)/shard_map/ppermute | solution.py:31
  217.7 13.4 %copy-start.8 = (f32[1024]{0:T(1024)S(1)}, f32[1024]{0:T(1024)}, u32[]{:S(2)}) copy-start(f32[1024]{0:T(1024)} %param.18) | copy-start | bytes 12292
  230.1 50.6 %copy-start.4 = (bf16[3,1024,64]{1,2,0:T(8,128)(2,1)S(1)}, bf16[3,1024,64]{1,2,0:T(8,128)(2,1)}, u32[]{:S(2)}) copy-start(bf16[3,1024,64]{1,2,0:T(8,128)(2,1)} %param.19) | copy-start | bytes 1179652
  232.0 130.1 %reduce-scatter.3.cloned.1.call-start = ((), (), s32[]{:S(2)}) async-start(), calls=%async_computation.5 | async-start | bytes 4456448 | tf_op jit(solution)/shard_map/reduce_scatter | solution.py:125
  285.5 11.4 %copy-start.5 = (bf16[64,1024]{1,0:T(8,128)(2,1)S(1)}, bf16[64,1024]{1,0:T(8,128)(2,1)}, u32[]{:S(2)}) copy-start(bf16[64,1024]{1,0:T(8,128)(2,1)} %param.20) | copy-start | bytes 393220
  300.1 64.2 %copy-start.9 = (f32[1024]{0:T(1024)S(1)}, f32[1024]{0:T(1024)}, u32[]{:S(2)}) copy-start(f32[1024]{0:T(1024)} %param.21) | copy-start | bytes 12292
  300.2 106.8 %copy-start.10 = (bf16[1024,256]{1,0:T(8,128)(2,1)S(1)}, bf16[1024,256]{1,0:T(8,128)(2,1)}, u32[]{:S(2)}) copy-start(bf16[1024,256]{1,0:T(8,128)(2,1)} %param.22) | copy-start | bytes 1572868
  300.2 106.8 %all-gather.5.cloned.1.call-start = ((), (), s32[]{:S(2)}) async-start(), calls=%async_computation.6 | async-start | bytes 4456448 | tf_op jit(solution)/shard_map/all_gather | solution.py:134
  366.2 111.2 %reduce-scatter.5.cloned.1.call-start = ((), (), s32[]{:S(2)}) async-start(), calls=%async_computation.7 | async-start | bytes 4456448 | tf_op jit(solution)/shard_map/reduce_scatter | solution.py:143
  415.5 62.0 %copy-start.1 = (bf16[128,1024]{1,0:T(8,128)(2,1)S(1)}, bf16[128,1024]{1,0:T(8,128)(2,1)}, u32[]{:S(2)}) copy-start(bf16[128,1024]{1,0:T(8,128)(2,1)} %reduce-scatter.3.cloned.1.call-done) | copy-start | bytes 786436
Sparse Core Ops, SparseCore 0:
  232.2 48.5 all-gather.2
  300.3 61.7 reduce-scatter.2
  366.3 40.6 all-gather.4
  415.6 61.7 reduce-scatter.4
